TPU v7x, 32 devices: a 4x4x1 block of a 4x4x8 slice. The times are simulated.
32 devices in a mesh: dp: 2 (over z, core), sp: 16 (over x, y).
Axes of the slice: x: 4, y: 4, z: 1, core: 2. Of those that a mesh axis runs over, the one named last changes fastest.
The devices are a block of a 4x4x8 slice.
Arguments:
- q: bfloat16 [64, 48, 128], P('dp'), parts along dimension 0
- k: bfloat16 [64, 8192, 8, 128], P('dp', 'sp'), parts along dimension 0
- v: bfloat16 [64, 8192, 8, 128], P('dp', 'sp'), parts along dimension 0
Outputs:
- q: bfloat16 [64, 48, 128], P('dp'), parts along dimension 0
There are 2 independent parts. A program takes and returns all parts, laid end to end along the dimension named above; each array names one.
All inputs are finite; a program needn't handle non-finite values.
Results may differ from a plain program's by a relative error of at most 0.012.
Values are sent between devices in bfloat16 or wider.
A program may use at most 768 MiB of HBM per device.

v0:
```python
import jax
import jax.numpy as jnp
from jax import lax
from jax.sharding import PartitionSpec as P


def einsum(form, a, b):
    return jnp.einsum(form, a.astype(jnp.float32), b.astype(jnp.float32))


def part_of(q, k, v):
    grouped = q.reshape(q.shape[0], k.shape[2], -1, q.shape[2])
    scores = einsum("bgsd,bugd->bgsu", grouped, k) * q.shape[2] ** -0.5
    high = jnp.max(scores, -1, keepdims=True)
    weights = jnp.exp(scores - high)
    seen = einsum("bgsu,bugd->bgsd", weights.astype(jnp.bfloat16), v)
    return jnp.concatenate([seen, jnp.sum(weights, -1, keepdims=True), high], -1)


def together(parts):
    seen, total, high = parts[..., :-2], parts[..., -2:-1], parts[..., -1:]
    scale = jnp.exp(high - jnp.max(high, 0))
    return (jnp.sum(seen * scale, 0) / jnp.sum(total * scale, 0)).astype(jnp.bfloat16)


def solution(mesh):
    def step(q, k, v):
        return together(lax.all_gather(part_of(q, k, v), "sp")).reshape(q.shape)

    return jax.shard_map(
        step,
        mesh=mesh,
        in_specs=(P("dp", None, None), P("dp", "sp", None, None), P("dp", "sp", None, None)),
        out_specs=P("dp", None, None),
        check_vma=False,
    )
```

profile of v0, /device:TPU:97, one launch (start us, length us, event | category | flops | bytes accessed | tf_op | source)
XLA Modules:
  0.0 254.4 jit_solution(11915627040344197153)
XLA Ops:
  6.5 0.0 all-gather.3.cloned.1.call-start
  6.6 1.1 copy.46
  7.7 14.4 %multiply_reduce_fusion = (f32[32,8,6]{2,1,0:T(8,128)S(1)}, f32[32,8,6,512]{3,2,1,0:T(8,128)S(1)}) fusion(bf16[32,512,8,128]{3,2,1,0:T(8,128)(2,1)} %param.4, bf16[32,8,6,128]{3,0,2,1:T(8,128)(2,1)S(1)} %bitcast.14), kind=kOutput, calls=%fused_computation.7 | convolution fusion | flops 202897920 | bytes 37099520 | tf_op jit(solution)/shard_map/bgsd,bugd->bgsu/dot_general | solution.py:8
  22.0 0.0 copy-start
  22.0 1.9 copy-done
  24.0 1.2 fusion.5
  25.1 16.2 %fusion = f32[32,8,6,128]{3,2,1,0:T(8,128)S(1)} fusion(bf16[32,512,8,128]{3,2,1,0:T(8,128)(2,1)} %param.5, f32[32,8,6,512]{3,2,1,0:T(8,128)} %copy-done, f32[32,8,6]{2,1,0:T(8,128)S(1)} %get-tuple-element.10), kind=kOutput, calls=%fused_computation | convolution fusion | flops 203685888 | bytes 37492736 | tf_op jit(solution)/shard_map/bgsu,bugd->bgsd/dot_general | solution.py:8
  41.4 1.7 copy.52
  43.1 1.7 copy.53
  44.7 0.4 pad_maximum_fusion
  45.1 1.9 copy.54
  47.0 0.1 all-gather.3.cloned.1.call-update
  47.1 152.7 %all-gather.3.cloned.1.call-done = f32[512,8,6,130]{3,1,2,0:T(8,128)} async-done(((f32[32,8,6,130]{3,1,2,0:T(8,128)}), f32[512,8,6,130]{3,1,2,0:T(8,128)}) %all-gather.3.cloned.1.call-update) | async-done | bytes 12779536 | tf_op jit(solution)/shard_map/all_gather | solution.py:28
  199.8 20.5 %fusion.14 = (f32[16,32,8,6,1]{4,2,3,1,0:T(8,128)}, f32[32,8,6]{1,2,0:T(8,128)S(1)}, f32[16,32,8,6,1]{4,2,3,1,0:T(8,128)}) fusion(f32[16,32,8,6,130]{4,2,3,1,0:T(8,128)} %bitcast.12), kind=kLoop, calls=%fused_computation.21 | loop fusion | flops 23040 | bytes 399360 | tf_op jit(solution)/shard_map/slice | solution.py:21
  220.3 8.5 %copy.68 = f32[16,32,8,6,1]{1,2,4,3,0:T(8,128)S(1)} copy(f32[16,32,8,6,1]{4,2,3,1,0:T(8,128)} %get-tuple-element.5) | data formatting | bytes 196608
  228.9 0.1 copy.70
  229.0 8.5 %copy.67 = f32[16,32,8,6,1]{1,2,4,3,0:T(8,128)S(1)} copy(f32[16,32,8,6,1]{4,2,3,1,0:T(8,128)} %get-tuple-element.7) | data formatting | bytes 196608
  237.5 0.1 multiply_reduce_fusion.1
  237.6 0.7 copy.56
  238.3 7.8 %fusion.4 = f32[32,8,6,128]{3,1,2,0:T(8,128)S(1)} fusion(f32[16,32,8,6,130]{4,2,3,1,0:T(8,128)} %bitcast.13, f32[16,32,8,6]{2,3,1,0:T(8,128)S(1)} %copy.56), kind=kLoop, calls=%fused_computation.5 | loop fusion | flops 6094848 | bytes 13467648 | tf_op jit(solution)/shard_map/reduce_sum | solution.py:23
  246.1 0.3 copy.58
  246.4 0.3 fusion.10
  246.6 0.9 copy.61
  (2 shorter events, 0.0 us)
Async XLA Ops:
  6.5 193.3 %all-gather.3.cloned.1.call-start = ((), (), s32[]{:S(2)}) async-start(), calls=%async_computation | async-start | bytes 26738688 | tf_op jit(solution)/shard_map/all_gather | solution.py:28
  22.0 1.9 copy-start
Sparse Core Ops, SparseCore 0:
  47.2 152.5 all-gather.2
where the time goes:
time: 255 us; the launch traced here: 254 us
  waiting for transfers between devices  153 us (60%)
  matrix products  30.6 us (12%)
  other arithmetic  30.2 us (12%)
  local copies, waits for them, and re-layouts  27.3 us (11%)
  between operations  13.5 us (5%)
    all_gather x1, waiting for transfers between devices, step(): return together(lax.all_gather(part_of(q, k, v), 'sp')).reshape(q.shape)  153 us
    dot_general x2, matrix products, einsum(): return jnp.einsum(form, a.astype(jnp.float32), b.astype(jnp.float32))  30.6 us
    slice x1, other arithmetic, together(): seen, total, high = (parts[..., :-2], parts[..., -2:-1], parts[..., -1:])  20.5 us
    unnamed x6, local copies, waits for them, and re-layouts  20.2 us
    reduce_sum x1, other arithmetic, together(): jnp.sum(seen * scale, 0) / jnp.sum(total * scale, 0)  7.76 us
  transfers between devices with their start and end apart: 1, of which 1 were waited for; matrix products, arithmetic and copies ran while one was open for 0% of the time, Pallas kernels for 0%

commit v1 on v0

v1 whole, which is shorter than its diff:
```python
import functools

import jax
import jax.numpy as jnp
from jax import lax
from jax.experimental import pallas as pl
from jax.experimental.pallas import tpu as pltpu
from jax.sharding import PartitionSpec as P

MESH = pl.DeviceIdType.MESH
LANES = 128
SUBLANES = 8
TILE = 256
SLOTS = 8
LAG = 6


def kernel(n, heads, q_hbm, k_hbm, v_hbm, out, qs, ks, vs, score_a, score_b, high_a, high_b, part, stat, got, got_stat, q_sem, k_sem, v_sem, part_send, part_recv, stat_send, stat_recv, out_send, out_recv):
    steps, rows, head = q_hbm.shape
    keys = k_hbm.shape[1]
    half = keys // 2
    share = rows // heads
    groups = rows // SUBLANES
    factor = head**-0.5 * 1.4426950408889634
    me = lax.axis_index("sp")

    lane = lax.broadcasted_iota(jnp.int32, (SUBLANES, LANES), 1)
    line = lax.broadcasted_iota(jnp.int32, (SUBLANES, LANES), 0)
    own = [lax.rem(lane, heads) == (line + SUBLANES * r) // share for r in range(groups)]
    wide = [jnp.concatenate([m] * (TILE // LANES), 1) for m in own]
    lane2 = lax.broadcasted_iota(jnp.int32, (2 * SUBLANES, TILE), 1)
    line2 = lax.broadcasted_iota(jnp.int32, (2 * SUBLANES, TILE), 0)
    keep = [jnp.where(lax.rem(lane2, heads) == (line2 + 2 * SUBLANES * r) // share, 1.0, 0.0).astype(jnp.bfloat16) for r in range(groups // 2)]
    low = lane < LANES // 2

    def sequence(s):
        return s // n * n + lax.rem(me + 1 + lax.rem(s, n), n)

    def k_copy(s):
        slot = lax.rem(s, SLOTS)
        return pltpu.make_async_copy(k_hbm.at[sequence(s)], ks.at[slot], k_sem.at[slot])

    def v_copy(s):
        slot = lax.rem(s, SLOTS)
        return pltpu.make_async_copy(v_hbm.at[sequence(s)], vs.at[slot], v_sem.at[slot])

    def part_copy(s):
        turn, j = s // n, lax.rem(s, n)
        owner = lax.rem(me + 1 + j, n)
        return (
            pltpu.make_async_remote_copy(part.at[s], got.at[turn, n - 2 - j], part_send, part_recv.at[turn], device_id={"sp": owner}, device_id_type=MESH),
            pltpu.make_async_remote_copy(stat.at[s], got_stat.at[turn, n - 2 - j], stat_send, stat_recv.at[turn], device_id={"sp": owner}, device_id_type=MESH),
        )

    def scores(s, score, high):
        slot = lax.rem(s, SLOTS)
        q = qs[sequence(s)]
        zero = jnp.zeros_like(q)
        both = jnp.concatenate([jnp.concatenate([q, zero], 1), jnp.concatenate([zero, q], 1)], 0)
        top = jnp.full((SUBLANES, LANES), -jnp.inf, jnp.float32)
        for c in range(half // TILE):
            block = jnp.concatenate([ks[slot, pl.ds(h * half + c * TILE, TILE), :] for h in range(2)], 1)
            all_scores = lax.dot_general(both, block, (((1,), (1,)), ((), ())), preferred_element_type=jnp.float32)
            for h in range(2):
                kept = jnp.full((SUBLANES, TILE), -jnp.inf, jnp.float32)
                for r in range(groups):
                    at = h * rows + r * SUBLANES
                    kept = jnp.where(wide[r], all_scores[at : at + SUBLANES], kept)
                score[h, :, pl.ds(c * TILE, TILE)] = kept
                for i in range(TILE // LANES):
                    top = jnp.maximum(top, kept[:, i * LANES : (i + 1) * LANES])
        high[...] = top

    def values(s, score, high):
        slot = lax.rem(s, SLOTS)
        top = high[...]
        high_row = jnp.zeros_like(top)
        for r in range(groups):
            high_row = jnp.where(own[r], jnp.max(jnp.where(own[r], top, -jnp.inf), 1, keepdims=True), high_row)
        high_wide = jnp.concatenate([high_row] * (TILE // LANES), 1)
        total = jnp.zeros_like(top)
        seen = None
        for c in range(half // TILE):
            weights = []
            for h in range(2):
                w = jnp.exp2((score[h, :, pl.ds(c * TILE, TILE)] - high_wide) * factor)
                for i in range(TILE // LANES):
                    total = total + w[:, i * LANES : (i + 1) * LANES]
                packed = jnp.concatenate([w, w], 0).astype(jnp.bfloat16)
                weights += [packed * m for m in keep]
            block = jnp.concatenate([vs[slot, pl.ds(h * half + c * TILE, TILE), :] for h in range(2)], 1)
            more = jnp.dot(jnp.concatenate(weights, 0), block, preferred_element_type=jnp.float32)
            seen = more if seen is None else seen + more
        total_row = jnp.zeros_like(top)
        for r in range(groups):
            total_row = jnp.where(own[r], jnp.sum(jnp.where(own[r], total, 0.0), 1, keepdims=True), total_row)
        stat[s] = jnp.where(low, high_row, total_row)
        part[s] = (seen[:rows, :head] + seen[rows:, head:]).astype(part.dtype)

    def send(s):
        @pl.when(lax.rem(s, n) != n - 1)
        def _():
            for copy in part_copy(s):
                copy.start()

    def together(turn):
        mine = turn * n + n - 1
        pltpu.make_async_remote_copy(got_stat.at[turn], got_stat.at[turn], stat_send, stat_recv.at[turn], device_id={"sp": me}, device_id_type=MESH).wait_recv()
        stats = [got_stat[turn, p] for p in range(n - 1)] + [stat[mine]]
        top = functools.reduce(jnp.maximum, stats)
        scale = [jnp.exp2((x - top) * factor) for x in stats]
        total = functools.reduce(jnp.add, [x * pltpu.roll(y, LANES // 2, 1) for x, y in zip(scale, stats)])
        scale = [x / total for x in scale]
        pltpu.make_async_remote_copy(got.at[turn], got.at[turn], part_send, part_recv.at[turn], device_id={"sp": me}, device_id_type=MESH).wait_recv()
        result = []
        for r in range(groups):
            first = jnp.logical_and(own[r], lane < heads)
            result.append([jnp.sum(jnp.where(first, x, 0.0), 1, keepdims=True) for x in scale])
        added = None
        for p in range(n):
            x = (got[turn, p] if p < n - 1 else part[mine]).astype(jnp.float32)
            x = x * jnp.concatenate([jnp.broadcast_to(result[r][p], (SUBLANES, head)) for r in range(groups)], 0)
            added = x if added is None else added + x
        at = turn * n + me
        out[at] = added.astype(out.dtype)
        for o in range(1, n):
            pltpu.make_async_remote_copy(out.at[at], out.at[at], out_send, out_recv.at[turn], device_id={"sp": lax.rem(me + o, n)}, device_id_type=MESH).start()

    barrier = pltpu.get_barrier_semaphore()
    pltpu.make_async_copy(q_hbm, qs, q_sem).start()
    for s in range(SLOTS):
        k_copy(s).start()
        v_copy(s).start()
    for o in range(1, n):
        pl.semaphore_signal(barrier, inc=1, device_id={"sp": lax.rem(me + o, n)}, device_id_type=MESH)
    pltpu.make_async_copy(q_hbm, qs, q_sem).wait()
    k_copy(0).wait()
    scores(0, score_a, high_a)
    k_copy(SLOTS).start()
    pl.semaphore_wait(barrier, n - 1)

    def turn_of(s, now, later, last=False):
        v_copy(s).wait()
        if not last:
            k_copy(s + 1).wait()
            scores(s + 1, *later)
        values(s, *now)

        @pl.when(s + SLOTS < steps)
        def _():
            v_copy(s + SLOTS).start()

        @pl.when(s + 1 + SLOTS < steps)
        def _():
            k_copy(s + 1 + SLOTS).start()

    first, second = (score_a, high_a), (score_b, high_b)

    def pair(t, _):
        s = 2 * t

        @pl.when(s > 0)
        def _():
            send(s - 1)

        turn_of(s, first, second)
        send(s)
        turn_of(s + 1, second, first)
        return 0

    at = 0
    for turn in range(steps // n - 1):
        to = ((turn + 1) * n + LAG) // 2
        lax.fori_loop(at, to, pair, 0)
        together(turn)
        at = to
    lax.fori_loop(at, steps // 2 - 1, pair, 0)
    s = steps - 2
    send(s - 1)
    turn_of(s, first, second)
    send(s)
    turn_of(s + 1, second, first, last=True)
    together(steps // n - 1)

    for turn in range(steps // n):
        block = out.at[pl.ds(0, n - 1)]
        pltpu.make_async_remote_copy(block, block, out_send, out_recv.at[turn], device_id={"sp": me}, device_id_type=MESH).wait()
        sent = part.at[pl.ds(0, n - 1)]
        pltpu.make_async_remote_copy(sent, sent, part_send, part_recv.at[turn], device_id={"sp": me}, device_id_type=MESH).wait_send()
        sent = stat.at[pl.ds(0, n - 1)]
        pltpu.make_async_remote_copy(sent, sent, stat_send, stat_recv.at[turn], device_id={"sp": me}, device_id_type=MESH).wait_send()


def attend(n, q, k, v):
    batch, rows, head = q.shape
    heads = k.shape[2]
    keys = k.shape[1] * heads
    turns = batch // n
    flat = (batch, keys, head)
    vmem = pltpu.VMEM
    dma = pltpu.SemaphoreType.DMA
    return pl.pallas_call(
        functools.partial(kernel, n, heads),
        out_shape=jax.ShapeDtypeStruct(q.shape, q.dtype),
        in_specs=[pl.BlockSpec(memory_space=pl.ANY)] * 3,
        out_specs=pl.BlockSpec(memory_space=vmem),
        scratch_shapes=[
            vmem(q.shape, q.dtype),
            vmem((SLOTS, keys, head), k.dtype),
            vmem((SLOTS, keys, head), v.dtype),
            vmem((2, SUBLANES, keys // 2), jnp.float32),
            vmem((2, SUBLANES, keys // 2), jnp.float32),
            vmem((SUBLANES, LANES), jnp.float32),
            vmem((SUBLANES, LANES), jnp.float32),
            vmem((batch, rows, head), q.dtype),
            vmem((batch, SUBLANES, LANES), jnp.float32),
            vmem((turns, n - 1, rows, head), q.dtype),
            vmem((turns, n - 1, SUBLANES, LANES), jnp.float32),
            dma,
            dma((SLOTS,)),
            dma((SLOTS,)),
            dma,
            dma((turns,)),
            dma,
            dma((turns,)),
            dma,
            dma((turns,)),
        ],
        compiler_params=pltpu.CompilerParams(collective_id=0, has_side_effects=True, vmem_limit_bytes=48 * 2**20),
        name="attend",
    )(q, k.reshape(flat), v.reshape(flat))


def solution(mesh):
    n = mesh.shape["sp"]
    return jax.shard_map(
        functools.partial(attend, n),
        mesh=mesh,
        in_specs=(P("dp", None, None), P("dp", "sp", None, None), P("dp", "sp", None, None)),
        out_specs=P("dp", None, None),
        check_vma=False,
    )
```

time: 255 us -> 39.2 us (0.15)
  waiting for transfers between devices: 153 us -> 0 us
  Pallas kernels: 0 us -> 36.9 us
  matrix products: 30.6 us -> 0 us
  other arithmetic: 30.2 us -> 0 us
  local copies, waits for them, and re-layouts: 27.3 us -> 1.74 us
  between operations: 13.5 us -> 0.01 us
    all_gather x1 -> x0, waiting for transfers between devices: 153 us -> none  [step(): return together(lax.all_gather(part_of(q, k, v), 'sp')).reshape(q.shape)]
    pallas_call x0 -> x1, Pallas kernels: none -> 36.9 us  [attend(): pl.pallas_call(functools.partial(kernel, n, heads), out_shape=jax.ShapeDt...]
    dot_general x2 -> x0, matrix products: 30.6 us -> none  [einsum(): return jnp.einsum(form, a.astype(jnp.float32), b.astype(jnp.float32))]
    slice x1 -> x0, other arithmetic: 20.5 us -> none  [together(): seen, total, high = (parts[..., :-2], parts[..., -2:-1], parts[..., -1:])]
    unnamed x6 -> x3, local copies, waits for them, and re-layouts: 20.2 us -> 1.74 us
    reduce_sum x3 -> x0, other arithmetic: 9.01 us -> none  [the longest x1 7.76 us: together(): jnp.sum(seen * scale, 0) / jnp.sum(total * scale, 0)]
    broadcast_in_dim x2 -> x0, local copies, waits for them, and re-layouts: 3.33 us -> none  [the longest x1 1.66 us: part_of(): high = jnp.max(scores, -1, keepdims=True)]
  transfers between devices with their start and end apart: 1 -> 0, of which waited for: 1 -> 0; matrix products, arithmetic and copies ran while one was open for 0% -> 0% of each run, Pallas kernels for 0% -> 0%
where the time goes in v1:
time: 39.2 us; the launch traced here: 38.6 us
  Pallas kernels  36.9 us (94%)
  local copies, waits for them, and re-layouts  1.74 us (4%)
    pallas_call x1, Pallas kernels, attend(): pl.pallas_call(functools.partial(kernel, n, heads), out_shape=jax.ShapeDt...  36.9 us
    unnamed x3, local copies, waits for them, and re-layouts  1.74 us

profile of v1, /device:TPU:97, one launch (start us, length us, event | category | flops | bytes accessed | tf_op | source)
XLA Modules:
  0.0 38.6 jit_solution(5254548354441353464)
XLA Ops:
  0.0 0.0 copy-start
  0.0 1.0 %copy-done = bf16[32,48,128]{2,1,0:T(8,128)(2,1)S(1)} copy-done((bf16[32,48,128]{2,1,0:T(8,128)(2,1)S(1)}, bf16[32,48,128]{2,1,0:T(8,128)(2,1)}, u32[]{:S(2)}) %copy-start) | copy-done | bytes 393240
  1.0 36.9 %attend.1 = bf16[32,48,128]{2,1,0:T(8,128)(2,1)S(1)} custom-call(bf16[32,48,128]{2,1,0:T(8,128)(2,1)S(1)} %copy-done, bf16[32,4096,128]{2,1,0:T(8,128)(2,1)} %bitcast.2, bf16[32,4096,128]{2,1,0:T(8,128)(2,1)} %bitcast.3), custom_call_target="tpu_custom_call" | custom-call | tf_op jit(solution)/shard_map/attend/pallas_call | solution.py:202
  37.9 0.7 %copy.5 = bf16[32,48,128]{2,1,0:T(8,128)(2,1)} copy(bf16[32,48,128]{2,1,0:T(8,128)(2,1)S(1)} %attend.1) | data formatting | bytes 786432
Async XLA Ops:
  0.0 1.0 %copy-start = (bf16[32,48,128]{2,1,0:T(8,128)(2,1)S(1)}, bf16[32,48,128]{2,1,0:T(8,128)(2,1)}, u32[]{:S(2)}) copy-start(bf16[32,48,128]{2,1,0:T(8,128)(2,1)} %q_hbm.1) | copy-start | bytes 1179652

commit v2 on v0

v2 whole, which is shorter than its diff:
```python
import functools
import math

import jax
import jax.numpy as jnp
from jax import lax
from jax.experimental import pallas as pl
from jax.experimental.pallas import tpu as pltpu
from jax.sharding import PartitionSpec as P

MESH = pl.DeviceIdType.MESH
LANES = 128
SUBLANES = 8
TILE = 256
DEPTH = 6
GREET = 3
WAIT = 5


def plan(batch, n):
    runs, at = [], 0
    while at < batch:
        owners = 1
        while at + n // owners > batch:
            owners *= 2
        runs.append((at, owners))
        at += n // owners
    return runs


def kernel(n, heads, runs, q_hbm, k_hbm, v_hbm, out, qs, ks, vs, score_a, score_b, high_a, high_b, weight_a, weight_b, part, part_stat, *rest):
    owned, owned_stat = rest[: len(runs)], rest[len(runs) : 2 * len(runs)]
    q_sem, k_sem, v_sem, owned_sent, owned_stat_sent, owned_came, owned_stat_came, out_sent, out_came = rest[2 * len(runs) :]
    batch, rows, head = q_hbm.shape
    pairs = batch // 2
    tail = (batch) // 2
    keys = k_hbm.shape[1]
    half = keys // 2
    share = rows // heads
    groups = rows // SUBLANES
    side = math.isqrt(n)
    factor = head**-0.5 * 1.4426950408889634
    me = lax.axis_index("sp")

    across, along = me // side, lax.rem(me, side)
    hops = [(abs(a - side // 2) + abs(b - side // 2), a, b) for a in range(side) for b in range(side) if a or b]
    others = [lax.rem(across + a, side) * side + lax.rem(along + b, side) for _, a, b in sorted(hops)]

    lane = lax.broadcasted_iota(jnp.int32, (SUBLANES, LANES), 1)
    line = lax.broadcasted_iota(jnp.int32, (SUBLANES, LANES), 0)
    own = [lax.rem(lane, heads) == (line + SUBLANES * r) // share for r in range(groups)]
    wide = [jnp.concatenate([m] * (TILE // LANES), 1) for m in own]
    lane2 = lax.broadcasted_iota(jnp.int32, (2 * SUBLANES, TILE), 1)
    line2 = lax.broadcasted_iota(jnp.int32, (2 * SUBLANES, TILE), 0)
    keep = [jnp.where(lax.rem(lane2, heads) == (line2 + 2 * SUBLANES * r) // share, 1.0, 0.0).astype(jnp.bfloat16) for r in range(groups // 2)]
    low = lane < LANES // 2

    def sequence(s):
        found = s
        for base, owners in reversed(runs):
            count = n // owners
            turned = base + lax.rem(me // owners + 1 + s - base, count)
            found = jnp.where(s < base + count, turned, found)
        return found

    def k_copies(t):
        slot = lax.rem(t, DEPTH)
        return [pltpu.make_async_copy(k_hbm.at[sequence(2 * t + i)], ks.at[slot, i], k_sem.at[slot, i]) for i in range(2)]

    def v_copies(t):
        slot = lax.rem(t, DEPTH)
        return [pltpu.make_async_copy(v_hbm.at[sequence(2 * t + i)], vs.at[slot, i], v_sem.at[slot, i]) for i in range(2)]

    def start(copies):
        for copy in copies:
            copy.start(priority=1)

    def wait(copies):
        for copy in copies:
            copy.wait()

    def scores(t, i, score, high):
        slot = lax.rem(t, DEPTH)
        q = qs[sequence(2 * t + i)]
        zero = jnp.zeros_like(q)
        both = jnp.concatenate([jnp.concatenate([q, zero], 1), jnp.concatenate([zero, q], 1)], 0)
        top = jnp.full((SUBLANES, LANES), -jnp.inf, jnp.float32)
        for c in range(half // TILE):
            block = jnp.concatenate([ks[slot, i, pl.ds(h * half + c * TILE, TILE), :] for h in range(2)], 1)
            all_scores = lax.dot_general(both, block, (((1,), (1,)), ((), ())), preferred_element_type=jnp.float32)
            for h in range(2):
                kept = jnp.full((SUBLANES, TILE), -jnp.inf, jnp.float32)
                for r in range(groups):
                    at = h * rows + r * SUBLANES
                    kept = jnp.where(wide[r], all_scores[at : at + SUBLANES], kept)
                score[h, :, pl.ds(c * TILE, TILE)] = kept
                for l in range(TILE // LANES):
                    top = jnp.maximum(top, kept[:, l * LANES : (l + 1) * LANES])
        high[...] = top

    def weights(t, i, score, high, weight):
        top = high[...]
        high_row = jnp.zeros_like(top)
        for r in range(groups):
            high_row = jnp.where(own[r], jnp.max(jnp.where(own[r], top, -jnp.inf), 1, keepdims=True), high_row)
        high_wide = jnp.concatenate([high_row] * (TILE // LANES), 1)
        total = jnp.zeros_like(top)
        for c in range(half // TILE):
            for h in range(2):
                w = jnp.exp2((score[h, :, pl.ds(c * TILE, TILE)] - high_wide) * factor)
                for l in range(TILE // LANES):
                    total = total + w[:, l * LANES : (l + 1) * LANES]
                packed = jnp.concatenate([w, w], 0).astype(jnp.bfloat16)
                for j, m in enumerate(keep):
                    weight[c, pl.ds(h * rows + 2 * SUBLANES * j, 2 * SUBLANES), :] = packed * m
        total_row = jnp.zeros_like(top)
        for r in range(groups):
            total_row = jnp.where(own[r], jnp.sum(jnp.where(own[r], total, 0.0), 1, keepdims=True), total_row)
        part_stat[2 * t + i] = jnp.where(low, high_row, total_row)

    def values(t, i, weight):
        slot = lax.rem(t, DEPTH)
        seen = None
        for c in range(half // TILE):
            block = jnp.concatenate([vs[slot, i, pl.ds(h * half + c * TILE, TILE), :] for h in range(2)], 1)
            more = jnp.dot(weight[c], block, preferred_element_type=jnp.float32)
            seen = more if seen is None else seen + more
        part[2 * t + i] = (seen[:rows, :head] + seen[rows:, head:]).astype(part.dtype)

    def give(run, q):
        base, owners = runs[run]
        size = rows // owners
        for i in range(owners):
            owner = lax.rem(me // owners + 1 + q - base, n // owners) * owners + i

            @pl.when(owner != me)
            def _():
                slot = lax.rem(me - owner + n, n) - 1
                pltpu.make_async_remote_copy(part.at[q, pl.ds(i * size, size)], owned[run].at[slot], owned_sent.at[run], owned_came.at[run], device_id={"sp": owner}, device_id_type=MESH).start()
                pltpu.make_async_remote_copy(part_stat.at[q], owned_stat[run].at[slot], owned_stat_sent.at[run], owned_stat_came.at[run], device_id={"sp": owner}, device_id_type=MESH).start()

    def together(run):
        base, owners = runs[run]
        size = rows // owners
        mine, place = base + n // owners - 1, base + me // owners
        at = lax.rem(me, owners) * size
        ours = pl.ds(pl.multiple_of(at, SUBLANES), size)
        for block, sem in ((owned_stat[run], owned_stat_came), (owned[run], owned_came)):
            pltpu.make_async_remote_copy(block, block, owned_sent.at[run], sem.at[run], device_id={"sp": me}, device_id_type=MESH).wait_recv()
        stat = [owned_stat[run][p] for p in range(n - 1)] + [part_stat[mine]]
        top = functools.reduce(jnp.maximum, stat)
        scale = [jnp.exp2((x - top) * factor) for x in stat]
        total = functools.reduce(jnp.add, [x * pltpu.roll(y, LANES // 2, 1) for x, y in zip(scale, stat)])
        scale = [x / total for x in scale]
        picks = [lane == (line + SUBLANES * r + at) // share for r in range(size // SUBLANES)]
        added = None
        for p, x in enumerate(scale):
            column = [jnp.broadcast_to(jnp.sum(jnp.where(f, x, 0.0), 1, keepdims=True), (SUBLANES, head)) for f in picks]
            more = (owned[run][p] if p < n - 1 else part[mine, ours]).astype(jnp.float32) * jnp.concatenate(column, 0)
            added = more if added is None else added + more
        out[place, ours] = added.astype(out.dtype)
        block = out.at[place, ours]
        for peer in others:
            pltpu.make_async_remote_copy(block, block, out_sent.at[run], out_came.at[run], device_id={"sp": peer}, device_id_type=MESH).start()

    q_copy = pltpu.make_async_copy(q_hbm, qs, q_sem)
    start(k_copies(0))
    q_copy.start()
    start(k_copies(1))
    for t in range(2, DEPTH):
        start(v_copies(t - 2))
        start(k_copies(t))
    for t in range(DEPTH - 2, DEPTH):
        start(v_copies(t))
    barrier = pltpu.get_barrier_semaphore()
    for o in range(1, n):
        pl.semaphore_signal(barrier, inc=1, device_id={"sp": lax.rem(me + o, n)}, device_id_type=MESH)
    scratch = ((score_a, high_a, weight_a), (score_b, high_b, weight_b))
    wait(k_copies(0))
    q_copy.wait()
    for i in range(2):
        scores(0, i, *scratch[i][:2])
    start(k_copies(DEPTH))
    wait(k_copies(1))
    for i in range(2):
        weights(0, i, *scratch[i])
    for i in range(2):
        scores(1, i, *scratch[i][:2])
    start(k_copies(DEPTH + 1))

    def share_out(t):
        run, t = t if isinstance(t, tuple) else (run_of(t), t)
        for i in range(2):
            give(run, 2 * t + i)

    def run_of(t):
        return max(run for run, (base, _) in enumerate(runs) if base <= 2 * t) if t < tail else None

    def step(run, t, _):
        if run != "nothing":
            share_out((run, t - 1))
        wait(v_copies(t))
        wait(k_copies(t + 2))
        for i in range(2):
            values(t, i, scratch[i][2])
        for i in range(2):
            weights(t + 1, i, *scratch[i])
        for i in range(2):
            scores(t + 2, i, *scratch[i][:2])

        @pl.when(t + DEPTH < pairs)
        def _():
            start(v_copies(t + DEPTH))

        @pl.when(t + 2 + DEPTH < pairs)
        def _():
            start(k_copies(t + 2 + DEPTH))

        return 0

    last = pairs - 1
    lax.fori_loop(0, GREET, functools.partial(step, "nothing"), 0)
    pl.semaphore_wait(barrier, n - 1)
    for t in range(GREET - 1):
        share_out(t)
    bounds = [base // 2 for base, _ in runs[1:]] + [tail]
    events = sorted([(end + 1, 0, run) for run, end in enumerate(bounds)] + [(end + WAIT, 1, run) for run, end in enumerate(bounds)])
    at, now, left = GREET, 0, list(range(len(runs)))
    for stop, kind, run in events:
        if stop < last:
            if stop > at:
                lax.fori_loop(at, stop, functools.partial(step, now), 0)
                at = stop
            if kind == 0:
                now = run + 1 if run + 1 < len(runs) else None
            else:
                together(run)
                left.remove(run)
    lax.fori_loop(at, last - 1, functools.partial(step, now), 0)
    share_out(last - 2)
    wait(v_copies(last - 1))
    for i in range(2):
        values(last - 1, i, scratch[i][2])
    for i in range(2):
        weights(last, i, *scratch[i])
    share_out(last - 1)
    for i in range(2):
        v_copies(last)[i].wait()
        values(last, i, scratch[i][2])
        give(run_of(last), 2 * last + i)
    for run in left:
        together(run)

    for run, (base, owners) in enumerate(runs):
        block = out.at[pl.ds(0, n - 1), pl.ds(0, rows // owners)]
        pltpu.make_async_remote_copy(block, block, out_sent.at[run], out_came.at[run], device_id={"sp": me}, device_id_type=MESH).wait()
        for block, sem in ((owned[run], owned_sent), (owned_stat[run], owned_stat_sent)):
            pltpu.make_async_remote_copy(block, block, sem.at[run], owned_came.at[run], device_id={"sp": me}, device_id_type=MESH).wait_send()


def attend(n, q, k, v):
    batch, rows, head = q.shape
    heads = k.shape[2]
    keys = k.shape[1] * heads
    runs = plan(batch, n)
    flat = (batch, keys, head)
    vmem = pltpu.VMEM
    dma = pltpu.SemaphoreType.DMA
    return pl.pallas_call(
        functools.partial(kernel, n, heads, runs),
        out_shape=jax.ShapeDtypeStruct(q.shape, q.dtype),
        in_specs=[pl.BlockSpec(memory_space=pltpu.HBM)] * 3,
        out_specs=pl.BlockSpec(memory_space=vmem),
        scratch_shapes=[
            vmem(q.shape, q.dtype),
            vmem((DEPTH, 2, keys, head), k.dtype),
            vmem((DEPTH, 2, keys, head), v.dtype),
            vmem((2, SUBLANES, keys // 2), jnp.float32),
            vmem((2, SUBLANES, keys // 2), jnp.float32),
            vmem((SUBLANES, LANES), jnp.float32),
            vmem((SUBLANES, LANES), jnp.float32),
            vmem((keys // 2 // TILE, 2 * rows, TILE), q.dtype),
            vmem((keys // 2 // TILE, 2 * rows, TILE), q.dtype),
            vmem((batch, rows, head), q.dtype),
            vmem((batch, SUBLANES, LANES), jnp.float32),
            *[vmem((n - 1, rows // owners, head), q.dtype) for _, owners in runs],
            *[vmem((n - 1, SUBLANES, LANES), jnp.float32) for _ in runs],
            dma,
            dma((DEPTH, 2)),
            dma((DEPTH, 2)),
            *[dma((len(runs),))] * 6,
        ],
        compiler_params=pltpu.CompilerParams(collective_id=0, has_side_effects=True, vmem_limit_bytes=52 * 2**20),
        name="attend",
    )(pltpu.with_memory_space_constraint(q, pltpu.HBM), k.reshape(flat), v.reshape(flat))


def solution(mesh):
    n = mesh.shape["sp"]
    return jax.shard_map(
        functools.partial(attend, n),
        mesh=mesh,
        in_specs=(P("dp", None, None), P("dp", "sp", None, None), P("dp", "sp", None, None)),
        out_specs=P("dp", None, None),
        check_vma=False,
    )
```

time: 255 us -> 37.2 us (0.15)
  waiting for transfers between devices: 153 us -> 0 us
  Pallas kernels: 0 us -> 36.2 us
  matrix products: 30.6 us -> 0 us
  other arithmetic: 30.2 us -> 0 us
  local copies, waits for them, and re-layouts: 27.3 us -> 0.75 us
  between operations: 13.5 us -> 0.01 us
    all_gather x1 -> x0, waiting for transfers between devices: 153 us -> none  [step(): return together(lax.all_gather(part_of(q, k, v), 'sp')).reshape(q.shape)]
    pallas_call x0 -> x1, Pallas kernels: none -> 36.2 us  [attend(): pl.pallas_call(functools.partial(kernel, n, heads, runs), out_shape=jax.S...]
    dot_general x2 -> x0, matrix products: 30.6 us -> none  [einsum(): return jnp.einsum(form, a.astype(jnp.float32), b.astype(jnp.float32))]
    slice x1 -> x0, other arithmetic: 20.5 us -> none  [together(): seen, total, high = (parts[..., :-2], parts[..., -2:-1], parts[..., -1:])]
    unnamed x6 -> x1, local copies, waits for them, and re-layouts: 20.2 us -> 0.75 us
    reduce_sum x3 -> x0, other arithmetic: 9.01 us -> none  [the longest x1 7.76 us: together(): jnp.sum(seen * scale, 0) / jnp.sum(total * scale, 0)]
    broadcast_in_dim x2 -> x0, local copies, waits for them, and re-layouts: 3.33 us -> none  [the longest x1 1.66 us: part_of(): high = jnp.max(scores, -1, keepdims=True)]
  transfers between devices with their start and end apart: 1 -> 0, of which waited for: 1 -> 0; matrix products, arithmetic and copies ran while one was open for 0% -> 0% of each run, Pallas kernels for 0% -> 0%
where the time goes in v2:
time: 37.2 us; the launch traced here: 36.9 us
  Pallas kernels  36.2 us (97%)
  local copies, waits for them, and re-layouts  0.75 us (2%)
    pallas_call x1, Pallas kernels, attend(): pl.pallas_call(functools.partial(kernel, n, heads, runs), out_shape=jax.S...  36.2 us
    unnamed x1, local copies, waits for them, and re-layouts  0.75 us

profile of v2, /device:TPU:97, one launch (start us, length us, event | category | flops | bytes accessed | tf_op | source)
XLA Modules:
  0.0 36.9 jit_solution(17415284855076386974)
XLA Ops:
  0.0 36.2 %attend.1 = bf16[32,48,128]{2,1,0:T(8,128)(2,1)S(1)} custom-call(bf16[32,48,128]{2,1,0:T(8,128)(2,1)} %q_hbm.1, bf16[32,4096,128]{2,1,0:T(8,128)(2,1)} %bitcast.2, bf16[32,4096,128]{2,1,0:T(8,128)(2,1)} %bitcast.3), custom_call_target="tpu_custom_call" | custom-call | tf_op jit(solution)/shard_map/attend/pallas_call | solution.py:269
  36.2 0.7 %copy.5 = bf16[32,48,128]{2,1,0:T(8,128)(2,1)} copy(bf16[32,48,128]{2,1,0:T(8,128)(2,1)S(1)} %attend.1) | data formatting | bytes 786432

commit v3 on v2

--- a/solution.py
+++ b/solution.py
@@ -13,8 +13,8 @@
 SUBLANES = 8
 TILE = 256
 DEPTH = 6
-GREET = 3
-WAIT = 5
+GREET = 2
+WAIT = 100
 
 
 def plan(batch, n):
@@ -127,7 +127,7 @@
             seen = more if seen is None else seen + more
         part[2 * t + i] = (seen[:rows, :head] + seen[rows:, head:]).astype(part.dtype)
 
-    def give(run, q):
+    def give(run, q, stats=True, values=True):
         base, owners = runs[run]
         size = rows // owners
         for i in range(owners):
@@ -136,8 +136,10 @@
             @pl.when(owner != me)
             def _():
                 slot = lax.rem(me - owner + n, n) - 1
-                pltpu.make_async_remote_copy(part.at[q, pl.ds(i * size, size)], owned[run].at[slot], owned_sent.at[run], owned_came.at[run], device_id={"sp": owner}, device_id_type=MESH).start()
-                pltpu.make_async_remote_copy(part_stat.at[q], owned_stat[run].at[slot], owned_stat_sent.at[run], owned_stat_came.at[run], device_id={"sp": owner}, device_id_type=MESH).start()
+                if stats:
+                    pltpu.make_async_remote_copy(part_stat.at[q], owned_stat[run].at[slot], owned_stat_sent.at[run], owned_stat_came.at[run], device_id={"sp": owner}, device_id_type=MESH).start()
+                if values:
+                    pltpu.make_async_remote_copy(part.at[q, pl.ds(i * size, size)], owned[run].at[slot], owned_sent.at[run], owned_came.at[run], device_id={"sp": owner}, device_id_type=MESH).start()
 
     def together(run):
         base, owners = runs[run]
@@ -145,17 +147,19 @@
         mine, place = base + n // owners - 1, base + me // owners
         at = lax.rem(me, owners) * size
         ours = pl.ds(pl.multiple_of(at, SUBLANES), size)
-        for block, sem in ((owned_stat[run], owned_stat_came), (owned[run], owned_came)):
-            pltpu.make_async_remote_copy(block, block, owned_sent.at[run], sem.at[run], device_id={"sp": me}, device_id_type=MESH).wait_recv()
+        block = owned_stat[run]
+        pltpu.make_async_remote_copy(block, block, owned_sent.at[run], owned_stat_came.at[run], device_id={"sp": me}, device_id_type=MESH).wait_recv()
         stat = [owned_stat[run][p] for p in range(n - 1)] + [part_stat[mine]]
         top = functools.reduce(jnp.maximum, stat)
         scale = [jnp.exp2((x - top) * factor) for x in stat]
         total = functools.reduce(jnp.add, [x * pltpu.roll(y, LANES // 2, 1) for x, y in zip(scale, stat)])
         scale = [x / total for x in scale]
         picks = [lane == (line + SUBLANES * r + at) // share for r in range(size // SUBLANES)]
+        columns = [[jnp.broadcast_to(jnp.sum(jnp.where(f, x, 0.0), 1, keepdims=True), (SUBLANES, head)) for f in picks] for x in scale]
+        block = owned[run]
+        pltpu.make_async_remote_copy(block, block, owned_sent.at[run], owned_came.at[run], device_id={"sp": me}, device_id_type=MESH).wait_recv()
         added = None
-        for p, x in enumerate(scale):
-            column = [jnp.broadcast_to(jnp.sum(jnp.where(f, x, 0.0), 1, keepdims=True), (SUBLANES, head)) for f in picks]
+        for p, column in enumerate(columns):
             more = (owned[run][p] if p < n - 1 else part[mine, ours]).astype(jnp.float32) * jnp.concatenate(column, 0)
             added = more if added is None else added + more
         out[place, ours] = added.astype(out.dtype)
@@ -245,9 +249,11 @@
         weights(last, i, *scratch[i])
     share_out(last - 1)
     for i in range(2):
+        give(run_of(last), 2 * last + i, values=False)
+    for i in range(2):
         v_copies(last)[i].wait()
         values(last, i, scratch[i][2])
-        give(run_of(last), 2 * last + i)
+        give(run_of(last), 2 * last + i, stats=False)
     for run in left:
         together(run)
 

time: 37.2 us -> 36.5 us (0.981)
  Pallas kernels: 36.2 us -> 35.6 us
    pallas_call x1, Pallas kernels: 36.2 us -> 35.6 us  [attend(): pl.pallas_call(functools.partial(kernel, n, heads, runs), out_shape=jax.S...]
where the time goes in v3:
time: 36.5 us; the launch traced here: 36.4 us
  Pallas kernels  35.6 us (98%)
  local copies, waits for them, and re-layouts  0.75 us (2%)
    pallas_call x1, Pallas kernels, attend(): pl.pallas_call(functools.partial(kernel, n, heads, runs), out_shape=jax.S...  35.6 us
    unnamed x1, local copies, waits for them, and re-layouts  0.75 us

profile of v3, /device:TPU:97, one launch (start us, length us, event | category | flops | bytes accessed | tf_op | source)
XLA Modules:
  0.0 36.4 jit_solution(3677439883822342773)
XLA Ops:
  0.0 35.6 %attend.1 = bf16[32,48,128]{2,1,0:T(8,128)(2,1)S(1)} custom-call(bf16[32,48,128]{2,1,0:T(8,128)(2,1)} %q_hbm.1, bf16[32,4096,128]{2,1,0:T(8,128)(2,1)} %bitcast.2, bf16[32,4096,128]{2,1,0:T(8,128)(2,1)} %bitcast.3), custom_call_target="tpu_custom_call" | custom-call | tf_op jit(solution)/shard_map/attend/pallas_call | solution.py:275
  35.6 0.7 %copy.5 = bf16[32,48,128]{2,1,0:T(8,128)(2,1)} copy(bf16[32,48,128]{2,1,0:T(8,128)(2,1)S(1)} %attend.1) | data formatting | bytes 786432
